TPU v7x, 32 devices: a whole 2x2x4 slice. The times are simulated.
32 devices in a mesh: img: 4 (over y, core), txt: 8 (over z, x).
Axes of the slice: x: 2, y: 2, z: 4, core: 2. Of those that a mesh axis runs over, the one named last changes fastest.
Arguments:
- queries: bfloat16 [1, 5120, 8192], P(None, 'txt', 'img'), may hold values from -128 to 128
- visual_keys: bfloat16 [1, 512, 8192], P(None, 'img'), may hold values from -5 to 5
- visual_values: bfloat16 [1, 512, 8192], P(None, 'img'), may hold values from -6 to 6
- out_grad: bfloat16 [1, 5120, 8192], P(None, 'txt', 'img'), may hold values from -6 to 6
- gate_value: float32 [1, 64], P(None, 'img'), may hold values from -1.5 to 1.5
- image_order: int32 [1, 8], replicated, may hold values from 0 to 7, as said below
- image_seen: int32 [5120], P('txt'), may hold values from 1 to 8
Outputs:
- query_grad: bfloat16 [1, 5120, 8192], P(None, 'txt', 'img')
- key_grad: float32 [1, 512, 8192], P(None, 'txt', 'img')
- value_grad: float32 [1, 512, 8192], P(None, 'txt', 'img')
Inputs may be any that keep to these rules, and one draw needn't show every extreme that they name: `image_order`: each row names every image of 0 to 7 once.
All inputs are finite; a program needn't handle non-finite values.
Results may differ from a plain program's by a relative error of at most 0.0058.
Values may be sent and summed in bfloat16 or wider, within the bound.
A program may use at most 128 MiB of HBM per device.

v0:
```python
import math
import jax
import jax.numpy as jnp
from jax import lax
from jax.sharding import PartitionSpec as P


def image_mask(order_row, image_seen, key_count):
    image_count = order_row.shape[0]
    latent_count = key_count // image_count
    key_image = jnp.broadcast_to(order_row[:, None], (image_count, latent_count)).reshape(key_count)
    return key_image[None, :] < image_seen[:, None]


def attention_grads(query, grad_in, factor, key_rows, value_rows, allowed, score_scale):
    token_count = query.shape[0]
    head_count = factor.shape[0]
    head_width = query.shape[1] // head_count
    key_count = key_rows.shape[0]
    query_heads = query.reshape(token_count, head_count, head_width)
    key_heads = key_rows.reshape(key_count, head_count, head_width)
    value_heads = value_rows.reshape(key_count, head_count, head_width)
    gated_grad = (
        grad_in.reshape(token_count, head_count, head_width).astype(jnp.float32)
        * factor[None, :, None]
    ).astype(jnp.bfloat16)
    scores = (
        jnp.einsum("thd,khd->htk", query_heads, key_heads, preferred_element_type=jnp.float32)
        * score_scale
    )
    masked = jnp.where(allowed[None], scores, -1e30)
    row_max = jnp.max(masked, axis=2, keepdims=True)
    exponent = jnp.where(allowed[None], jnp.exp(masked - row_max), 0.0)
    weights = exponent / jnp.sum(exponent, axis=2, keepdims=True)
    weight_half = weights.astype(jnp.bfloat16)
    attended = jnp.einsum(
        "htk,khd->thd", weight_half, value_heads, preferred_element_type=jnp.float32
    )
    row_delta = jnp.sum(gated_grad.astype(jnp.float32) * attended, axis=2)
    weight_grad = jnp.einsum(
        "thd,khd->htk", gated_grad, value_heads, preferred_element_type=jnp.float32
    )
    score_half = (weights * (weight_grad - jnp.transpose(row_delta)[:, :, None])).astype(
        jnp.bfloat16
    )
    query_part = (
        jnp.einsum("htk,khd->thd", score_half, key_heads, preferred_element_type=jnp.float32)
        * score_scale
    )
    return (
        query_part.astype(jnp.bfloat16).reshape(token_count, -1),
        score_half,
        weight_half,
        query_heads,
        gated_grad,
    )


def latent_terms(score_half, weight_half, query_heads, gated_grad, count, score_scale):
    key_part = (
        jnp.einsum("htk,thd->khd", score_half, query_heads, preferred_element_type=jnp.float32)
        * score_scale
    )
    value_part = jnp.einsum(
        "htk,thd->khd", weight_half, gated_grad, preferred_element_type=jnp.float32
    )
    return (key_part.reshape(count, -1), value_part.reshape(count, -1))


def shards(queries, visual_keys, visual_values, out_grad, gate_value, image_order, image_seen):
    width_local = queries.shape[2]
    head_width = width_local // gate_value.shape[1]
    score_scale = 1.0 / math.sqrt(head_width)
    key_rows = lax.all_to_all(visual_keys[0], "img", split_axis=1, concat_axis=0, tiled=True)
    value_rows = lax.all_to_all(visual_values[0], "img", split_axis=1, concat_axis=0, tiled=True)
    key_total = key_rows.shape[0]
    allowed = image_mask(image_order[0], image_seen, key_total)
    factor = jnp.tanh(gate_value[0])
    query_part, score_half, weight_half, query_heads, gated_grad = attention_grads(
        queries[0], out_grad[0], factor, key_rows, value_rows, allowed, score_scale
    )
    query_list = [query_part]
    key_part, value_part = latent_terms(
        score_half, weight_half, query_heads, gated_grad, key_total, score_scale
    )
    key_share = lax.psum_scatter(key_part, "txt", scatter_dimension=0, tiled=True)
    value_share = lax.psum_scatter(value_part, "txt", scatter_dimension=0, tiled=True)
    key_list = [key_share]
    value_list = [value_share]
    key_grad = jnp.stack(key_list)
    value_grad = jnp.stack(value_list)
    return (jnp.stack(query_list), key_grad, value_grad)


def solution(mesh):
    placed = (
        P(None, "txt", "img"),
        P(None, "img", None),
        P(None, "img", None),
        P(None, "txt", "img"),
        P(None, "img"),
        P(),
        P("txt"),
    )
    return jax.shard_map(
        shards,
        mesh=mesh,
        in_specs=placed,
        out_specs=(P(None, "txt", "img"), P(None, "txt", "img"), P(None, "txt", "img")),
        check_vma=False,
    )
```

profile of v0, /device:TPU:0, one launch (start us, length us, event | category | flops | bytes accessed | tf_op | source)
XLA Modules:
  0.0 274.3 jit_solution(15759420821382776960)
XLA Ops:
  7.2 3.3 %all_to_all.24 = bf16[128,4,2048]{2,1,0:T(4,128)(2,1)S(1)} reshape(bf16[1,128,8192]{2,1,0:T(8,128)(2,1)} %param.8) | data formatting | bytes 4194304 | tf_op jit(solution)/shard_map/all_to_all | solution.py:74
  10.5 2.5 copy.24
  13.0 4.7 %all-to-all-start = ((bf16[128,4,2048]{2,0,1:T(8,128)(2,1)}), bf16[128,4,2048]{2,0,1:T(8,128)(2,1)}, u32[]{:S(2)}, u32[]{:S(2)}) async-start(bf16[128,4,2048]{2,0,1:T(8,128)(2,1)} %copy.24), calls=%async_computation | async-start | bytes 4194304 | tf_op jit(solution)/shard_map/all_to_all | solution.py:74
  17.8 0.0 reduce-scatter.5.cloned.1.call-start
  17.8 0.1 broadcast_in_dim.33
  17.9 0.1 lt.19
  18.0 2.6 copy.48
  20.5 4.9 %copy.27 = f32[1,640,2048]{1,2,0:T(8,128)} copy(bf16[1,640,2048]{2,1,0:T(8,128)(2,1)} %param.10) | data formatting | bytes 7864320 | tf_op jit(solution)/shard_map/convert_element_type | solution.py:24
  25.5 0.3 broadcast_compare_fusion
  25.7 3.1 %multiply_convert_fusion.2 = bf16[640,16,128]{0,2,1:T(8,128)(2,1)S(1)} fusion(f32[640,16,128]{0,2,1:T(8,128)} %bitcast.43, f32[16]{0:T(128)S(1)} %tanh_bitcast_fusion), kind=kLoop, calls=%fused_computation.13 | loop fusion | flops 2621440 | bytes 7864384 | tf_op jit(solution)/shard_map/convert_element_type | solution.py:26
  28.8 15.4 %all-to-all-done = bf16[128,4,2048]{2,0,1:T(8,128)(2,1)} async-done(((bf16[128,4,2048]{2,0,1:T(8,128)(2,1)}), bf16[128,4,2048]{2,0,1:T(8,128)(2,1)}, u32[]{:S(2)}, u32[]{:S(2)}) %all-to-all-start) | async-done | bytes 2097184 | tf_op jit(solution)/shard_map/all_to_all | solution.py:74
  44.2 3.6 %copy.49 = bf16[64,8,16,128]{3,2,1,0:T(8,128)(2,1)} copy(bf16[64,8,16,128]{3,1,2,0:T(8,128)(2,1)} %bitcast.20) | data formatting | bytes 4194304
  47.8 4.3 %copy.35 = bf16[512,16,128]{0,2,1:T(8,128)(2,1)} copy(bf16[512,16,128]{2,1,0:T(8,128)(2,1)} %bitcast.49) | data formatting | bytes 4194304 | tf_op jit(solution)/shard_map/reshape | solution.py:21
  52.1 14.4 %fusion.11 = (f32[16,640]{1,0:T(8,128)S(1)}, f32[16,640,512]{1,2,0:T(8,128)}) fusion(pred[640,512]{0,1:T(8,128)(4,1)S(1)} %broadcast_compare_fusion, bf16[640,16,128]{0,2,1:T(8,128)(2,1)} %bitcast.47, bf16[512,16,128]{0,2,1:T(8,128)(2,1)} %copy.35), kind=kOutput, calls=%fused_computation.20 | convolution fusion | flops 1368392192 | bytes 26058752 | tf_op jit(solution)/shard_map/sub | solution.py:33
  66.4 8.5 %fusion.5 = bf16[16,640,512]{1,2,0:T(8,128)(2,1)S(1)} fusion(f32[16,640,512]{1,2,0:T(8,128)} %get-tuple-element.10, f32[16,640]{1,0:T(8,128)S(1)} %get-tuple-element.9), kind=kLoop, calls=%fused_computation.9 | loop fusion | flops 10485760 | bytes 31498240 | tf_op jit(solution)/shard_map/convert_element_type | solution.py:35
  75.0 5.3 %fusion.12 = f32[16,128,512]{2,1,0:T(8,128)} fusion(bf16[640,16,128]{0,2,1:T(8,128)(2,1)S(1)} %multiply_convert_fusion.2, bf16[16,640,512]{1,2,0:T(8,128)(2,1)S(1)} %fusion.5), kind=kOutput, calls=%fused_computation.21 | convolution fusion | flops 1342177280 | bytes 17301504 | tf_op jit(solution)/shard_map/htk,thd->khd/dot_general | solution.py:64
  80.3 5.4 %copy.40 = f32[512,2048]{1,0:T(8,128)} copy(f32[512,2048]{0,1:T(8,128)} %bitcast.46) | data formatting | bytes 8388608 | tf_op jit(solution)/shard_map/reshape | solution.py:67
  85.7 0.0 reduce-scatter.5.cloned.1.call-update
  85.8 0.2 reduce-scatter.3.cloned.1.call-start
  86.0 4.5 %all_to_all.27 = bf16[128,4,2048]{2,1,0:T(4,128)(2,1)} reshape(bf16[1,128,8192]{2,1,0:T(8,128)(2,1)} %param.9) | data formatting | bytes 4194304 | tf_op jit(solution)/shard_map/all_to_all | solution.py:75
  90.5 2.7 %copy.28 = bf16[128,4,2048]{2,0,1:T(8,128)(2,1)S(1)} copy(bf16[128,4,2048]{2,1,0:T(4,128)(2,1)} %all_to_all.27) | data formatting | bytes 4194304 | tf_op jit(solution)/shard_map/all_to_all | solution.py:75
  93.3 28.1 %all_to_all.32 = bf16[128,4,2048]{2,0,1:T(8,128)(2,1)S(1)} all-to-all(bf16[128,4,2048]{2,0,1:T(8,128)(2,1)S(1)} %copy.28), channel_id=1, replica_groups=mesh['img'=4,'txt'=8] {'img'}, dimensions={1} | all-to-all | bytes 4194304 | tf_op jit(solution)/shard_map/all_to_all | solution.py:75
  121.4 1.9 copy.50
  123.3 4.3 %copy.32 = bf16[512,16,128]{0,2,1:T(8,128)(2,1)} copy(bf16[512,16,128]{2,1,0:T(8,128)(2,1)} %bitcast.51) | data formatting | bytes 4194304 | tf_op jit(solution)/shard_map/reshape | solution.py:22
  127.7 6.8 %fusion.6 = f32[640,16]{0,1:T(8,128)S(1)} fusion(bf16[640,16,128]{0,2,1:T(8,128)(2,1)S(1)} %multiply_convert_fusion.2, bf16[512,16,128]{0,2,1:T(8,128)(2,1)} %copy.32, bf16[16,640,512]{1,2,0:T(8,128)(2,1)} %copy-done), kind=kOutput, calls=%fused_computation.11 | convolution fusion | flops 1346099200 | bytes 15245312 | tf_op jit(solution)/shard_map/htk,khd->thd/dot_general | solution.py:36
  134.5 12.5 %multiply_convert_fusion = bf16[16,640,512]{1,2,0:T(8,128)(2,1)} fusion(f32[16,640]{1,0:T(8,128)S(1)} %bitcast.52, f32[16,640,512]{1,2,0:T(8,128)} %get-tuple-element.10, f32[16,640]{1,0:T(8,128)S(1)} %get-tuple-element.9, bf16[512,16,128]{0,2,1:T(8,128)(2,1)S(1)} %copy-done.1, bf16[640,16,128]{0,2,1:T(8,128)(2,1)S(1)} %multiply_convert_fusion.2), kind=kOutput, calls=%fused_computation.1 | convolution fusion | flops 1363148800 | bytes 36257792 | tf_op jit(solution)/shard_map/thd,khd->htk/dot_general | solution.py:40
  147.0 10.1 %broadcast_multiply_fusion = f32[16,512,128]{1,2,0:T(8,128)} fusion(bf16[16,640,512]{1,2,0:T(8,128)(2,1)} %multiply_convert_fusion, bf16[640,16,128]{0,2,1:T(8,128)(2,1)} %bitcast.48), kind=kOutput, calls=%fused_computation.14 | convolution fusion | flops 1343225856 | bytes 17301504 | tf_op jit(solution)/shard_map/htk,thd->khd/dot_general | solution.py:61
  157.0 5.4 %copy.38 = f32[512,2048]{1,0:T(8,128)} copy(f32[512,2048]{0,1:T(8,128)} %bitcast.45) | data formatting | bytes 8388608 | tf_op jit(solution)/shard_map/reshape | solution.py:67
  162.5 6.6 %multiply_convert_fusion.1 = bf16[16,640,128]{1,2,0:T(8,128)(2,1)S(1)} fusion(bf16[512,16,128]{0,2,1:T(8,128)(2,1)} %copy.35, bf16[16,640,512]{1,2,0:T(8,128)(2,1)} %multiply_convert_fusion), kind=kOutput, calls=%fused_computation.12 | convolution fusion | flops 1344798720 | bytes 15204352 | tf_op jit(solution)/shard_map/htk,khd->thd/dot_general | solution.py:47
  169.1 2.6 copy.41
  171.7 3.6 %reduce-scatter.5.cloned.1.call-done = f32[64,2048]{1,0:T(8,128)} async-done(((f32[512,2048]{1,0:T(8,128)}), f32[64,2048]{1,0:T(8,128)}) %reduce-scatter.5.cloned.1.call-update) | async-done | bytes 524304 | tf_op jit(solution)/shard_map/reduce_scatter | solution.py:87
  175.3 92.2 %reduce-scatter.3.cloned.1.call-done = f32[64,2048]{1,0:T(8,128)} async-done(((f32[512,2048]{1,0:T(8,128)}), f32[64,2048]{1,0:T(8,128)}) %reduce-scatter.3.cloned.1.call-update) | async-done | bytes 524304 | tf_op jit(solution)/shard_map/reduce_scatter | solution.py:86
  (14 shorter events, 0.0 us)
Async XLA Ops:
  10.5 7.3 %copy-start.4 = (s32[1,8]{1,0:T(1,128)S(1)}, s32[1,8]{1,0:T(1,128)}, u32[]{:S(2)}) copy-start(s32[1,8]{1,0:T(1,128)} %param.12) | copy-start | bytes 100
  13.0 4.9 %copy-start.2 = (bf16[1,640,2048]{2,1,0:T(8,128)(2,1)S(1)}, bf16[1,640,2048]{2,1,0:T(8,128)(2,1)}, u32[]{:S(2)}) copy-start(bf16[1,640,2048]{2,1,0:T(8,128)(2,1)} %param.7) | copy-start | bytes 7864324
  13.0 31.2 %all-to-all-start = ((bf16[128,4,2048]{2,0,1:T(8,128)(2,1)}), bf16[128,4,2048]{2,0,1:T(8,128)(2,1)}, u32[]{:S(2)}, u32[]{:S(2)}) async-start(bf16[128,4,2048]{2,0,1:T(8,128)(2,1)} %copy.24), calls=%async_computation | async-start | bytes 4194304 | tf_op jit(solution)/shard_map/all_to_all | solution.py:74
  17.8 157.5 %reduce-scatter.5.cloned.1.call-start = ((), (), s32[]{:S(2)}) async-start(), calls=%async_computation.5 | async-start | bytes 4718592 | tf_op jit(solution)/shard_map/reduce_scatter | solution.py:87
  20.5 4.9 %copy-start.5 = (f32[1,16]{1,0:T(1,128)S(1)}, f32[1,16]{1,0:T(1,128)}, u32[]{:S(2)}) copy-start(f32[1,16]{1,0:T(1,128)} %param.11) | copy-start | bytes 196
  20.5 4.9 %copy-start.3 = (s32[640]{0:T(1024)S(1)}, s32[640]{0:T(1024)}, u32[]{:S(2)}) copy-start(s32[640]{0:T(1024)} %param.13) | copy-start | bytes 7684
  75.0 5.3 %copy-start = (bf16[16,640,512]{1,2,0:T(8,128)(2,1)}, bf16[16,640,512]{1,2,0:T(8,128)(2,1)S(1)}, u32[]{:S(2)}) copy-start(bf16[16,640,512]{1,2,0:T(8,128)(2,1)S(1)} %fusion.5) | copy-start | bytes 31457284
  85.8 181.7 %reduce-scatter.3.cloned.1.call-start = ((), (), s32[]{:S(2)}) async-start(), calls=%async_computation.4 | async-start | bytes 4718592 | tf_op jit(solution)/shard_map/reduce_scatter | solution.py:86
  127.7 6.8 %copy-start.1 = (bf16[512,16,128]{0,2,1:T(8,128)(2,1)S(1)}, bf16[512,16,128]{0,2,1:T(8,128)(2,1)}, u32[]{:S(2)}) copy-start(bf16[512,16,128]{0,2,1:T(8,128)(2,1)} %copy.32) | copy-start | bytes 6291460
Sparse Core Ops, SparseCore 0:
  85.9 89.3 reduce-scatter.4
  179.5 87.9 reduce-scatter.2
where the time goes:
time: 275 us; the launch traced here: 274 us
  waiting for transfers between devices  111 us (40%)
  matrix products  55.7 us (20%)
  local copies, waits for them, and re-layouts  48.4 us (18%)
  blocking collectives  28.1 us (10%)
  between operations  14.1 us (5%)
  other arithmetic  11.9 us (4%)
  starting transfers between devices  4.98 us (2%)
    reduce_scatter x1, waiting for transfers between devices, shards(): lax.psum_scatter(key_part, 'txt', scatter_dimension=0, tiled=True)  92.2 us
    all_to_all x1, blocking collectives, shards(): lax.all_to_all(visual_values[0], 'img', split_axis=1, concat_axis=0, tile...  28.1 us
    all_to_all x1, waiting for transfers between devices, shards(): lax.all_to_all(visual_keys[0], 'img', split_axis=1, concat_axis=0, tiled=...  15.4 us
    sub x1, matrix products, attention_grads(): exponent = jnp.where(allowed[None], jnp.exp(masked - row_max), 0.0)  14.4 us
    dot_general x1, matrix products, attention_grads(): jnp.einsum('thd,khd->htk', gated_grad, value_heads, preferred_element_typ...  12.5 us
    reshape x2, local copies, waits for them, and re-layouts, latent_terms(): return (key_part.reshape(count, -1), value_part.reshape(count, -1))  10.8 us
    dot_general x1, matrix products, latent_terms(): jnp.einsum('htk,thd->khd', score_half, query_heads, preferred_element_typ...  10.1 us
    convert_element_type x1, other arithmetic, attention_grads(): weight_half = weights.astype(jnp.bfloat16)  8.53 us
  transfers between devices with their start and end apart: 3, of which 3 were waited for; matrix products, arithmetic and copies ran while one was open for 23% of the time, Pallas kernels for 0%

commit v1 on v0

--- a/solution.py
+++ b/solution.py
@@ -71,7 +71,11 @@
     width_local = queries.shape[2]
     head_width = width_local // gate_value.shape[1]
     score_scale = 1.0 / math.sqrt(head_width)
-    key_rows = lax.all_to_all(visual_keys[0], "img", split_axis=1, concat_axis=0, tiled=True)
+    own = visual_keys[0]
+    n_dev = lax.axis_size("img")
+    parts = jnp.stack(jnp.split(own, n_dev, axis=1), axis=0)
+    parts = lax.all_to_all(parts, "img", split_axis=0, concat_axis=0)
+    key_rows = jnp.concatenate(parts, axis=0)
     value_rows = lax.all_to_all(visual_values[0], "img", split_axis=1, concat_axis=0, tiled=True)
     key_total = key_rows.shape[0]
     allowed = image_mask(image_order[0], image_seen, key_total)

time: 275 us -> 272 us (0.989)
  local copies, waits for them, and re-layouts: 48.4 us -> 44.2 us
    another operation x0 -> x2, local copies, waits for them, and re-layouts: none -> 5.98 us  [the longest x1 4.32 us: attention_grads(): key_heads = key_rows.reshape(key_count, head_count, head_width)]
    all_to_all x2 -> x0, local copies, waits for them, and re-layouts: 5.85 us -> none  [shards(): lax.all_to_all(visual_keys[0], 'img', split_axis=1, concat_axis=0, tiled=...]
    reshape x1 -> x0, local copies, waits for them, and re-layouts: 4.31 us -> none  [attention_grads(): key_heads = key_rows.reshape(key_count, head_count, head_width)]
  transfers between devices with their start and end apart: 3 -> 3, of which waited for: 3 -> 3; matrix products, arithmetic and copies ran while one was open for 23% -> 24% of each run, Pallas kernels for 0% -> 0%
where the time goes in v1:
time: 272 us
  waiting for transfers between devices  111 us (41%)
  matrix products  55.6 us (20%)
  local copies, waits for them, and re-layouts  44.2 us (16%)
  blocking collectives  28.1 us (10%)
  between operations  14.1 us (5%)
  other arithmetic  13.5 us (5%)
  starting transfers between devices  4.54 us (2%)
    reduce_scatter x1, waiting for transfers between devices, shards(): lax.psum_scatter(key_part, 'txt', scatter_dimension=0, tiled=True)  92.2 us
    all_to_all x1, blocking collectives, shards(): lax.all_to_all(visual_values[0], 'img', split_axis=1, concat_axis=0, tile...  28.1 us
    all_to_all x1, waiting for transfers between devices, shards(): parts = lax.all_to_all(parts, 'img', split_axis=0, concat_axis=0)  15.4 us
    sub x1, matrix products, attention_grads(): exponent = jnp.where(allowed[None], jnp.exp(masked - row_max), 0.0)  14.4 us
    dot_general x1, matrix products, attention_grads(): jnp.einsum('thd,khd->htk', gated_grad, value_heads, preferred_element_typ...  12.4 us
    reshape x2, local copies, waits for them, and re-layouts, latent_terms(): return (key_part.reshape(count, -1), value_part.reshape(count, -1))  10.9 us
    dot_general x1, matrix products, latent_terms(): jnp.einsum('htk,thd->khd', score_half, query_heads, preferred_element_typ...  10.1 us
    convert_element_type x1, other arithmetic, attention_grads(): weight_half = weights.astype(jnp.bfloat16)  8.56 us
  transfers between devices with their start and end apart: 3, of which 3 were waited for; matrix products, arithmetic and copies ran while one was open for 24% of the time, Pallas kernels for 0%

profile of v1, /device:TPU:0, one launch (start us, length us, event | category | flops | bytes accessed | tf_op | source)
XLA Modules:
  0.0 271.5 jit_solution(15400720024568650520)
XLA Ops:
  7.2 1.7 slice_bitcast_fusion.3
  8.8 1.6 pad_maximum_fusion
  10.5 4.5 %all-to-all-start = ((bf16[4,128,2048]{2,1,0:T(8,128)(2,1)}), bf16[4,128,2048]{2,1,0:T(8,128)(2,1)}, u32[]{:S(2)}, u32[]{:S(2)}) async-start(bf16[4,128,2048]{2,1,0:T(8,128)(2,1)} %pad_maximum_fusion), calls=%async_computation | async-start | bytes 4194304 | tf_op jit(solution)/shard_map/all_to_all | solution.py:77
  15.0 0.0 reduce-scatter.5.cloned.1.call-start
  15.0 0.1 broadcast_in_dim.33
  15.1 0.1 lt.19
  15.2 2.6 copy.47
  17.7 4.9 %copy.26 = f32[1,640,2048]{1,2,0:T(8,128)} copy(bf16[1,640,2048]{2,1,0:T(8,128)(2,1)} %param.10) | data formatting | bytes 7864320 | tf_op jit(solution)/shard_map/convert_element_type | solution.py:24
  22.7 0.3 broadcast_compare_fusion
  22.9 3.1 %multiply_convert_fusion.2 = bf16[640,16,128]{0,2,1:T(8,128)(2,1)S(1)} fusion(f32[640,16,128]{0,2,1:T(8,128)} %bitcast.62, f32[16]{0:T(128)S(1)} %tanh_bitcast_fusion), kind=kLoop, calls=%fused_computation.13 | loop fusion | flops 2621440 | bytes 7864384 | tf_op jit(solution)/shard_map/convert_element_type | solution.py:26
  26.0 15.4 %all-to-all-done = bf16[4,128,2048]{2,1,0:T(8,128)(2,1)} async-done(((bf16[4,128,2048]{2,1,0:T(8,128)(2,1)}), bf16[4,128,2048]{2,1,0:T(8,128)(2,1)}, u32[]{:S(2)}, u32[]{:S(2)}) %all-to-all-start) | async-done | bytes 2097184 | tf_op jit(solution)/shard_map/all_to_all | solution.py:77
  41.4 3.6 %copy.48 = bf16[64,8,16,128]{3,2,1,0:T(8,128)(2,1)} copy(bf16[64,8,16,128]{3,1,2,0:T(8,128)(2,1)} %bitcast.25) | data formatting | bytes 4194304
  44.9 4.3 %copy.33 = bf16[512,16,128]{0,2,1:T(8,128)(2,1)} copy(bf16[512,16,128]{2,1,0:T(8,128)(2,1)} %bitcast.68) | data formatting | bytes 4194304 | tf_op jit(solution)/shard_map/reshape;reshape | solution.py:21
  49.3 14.4 %fusion.11 = (f32[16,640]{1,0:T(8,128)S(1)}, f32[16,640,512]{1,2,0:T(8,128)}) fusion(pred[640,512]{0,1:T(8,128)(4,1)S(1)} %broadcast_compare_fusion, bf16[512,16,128]{0,2,1:T(8,128)(2,1)} %copy.33, bf16[640,16,128]{0,2,1:T(8,128)(2,1)} %bitcast.66), kind=kOutput, calls=%fused_computation.25 | convolution fusion | flops 1368392192 | bytes 26058752 | tf_op jit(solution)/shard_map/sub | solution.py:33
  63.6 8.6 %fusion.5 = bf16[16,640,512]{1,2,0:T(8,128)(2,1)S(1)} fusion(f32[16,640,512]{1,2,0:T(8,128)} %get-tuple-element.14, f32[16,640]{1,0:T(8,128)S(1)} %get-tuple-element.13), kind=kLoop, calls=%fused_computation.9 | loop fusion | flops 10485760 | bytes 31498240 | tf_op jit(solution)/shard_map/convert_element_type | solution.py:35
  72.2 5.3 %fusion.12 = f32[16,128,512]{2,1,0:T(8,128)} fusion(bf16[640,16,128]{0,2,1:T(8,128)(2,1)S(1)} %multiply_convert_fusion.2, bf16[16,640,512]{1,2,0:T(8,128)(2,1)S(1)} %fusion.5), kind=kOutput, calls=%fused_computation.26 | convolution fusion | flops 1342177280 | bytes 17301504 | tf_op jit(solution)/shard_map/htk,thd->khd/dot_general | solution.py:64
  77.5 5.4 %copy.39 = f32[512,2048]{1,0:T(8,128)} copy(f32[512,2048]{0,1:T(8,128)} %bitcast.65) | data formatting | bytes 8388608 | tf_op jit(solution)/shard_map/reshape | solution.py:67
  82.9 0.0 reduce-scatter.5.cloned.1.call-update
  83.0 0.0 reduce-scatter.3.cloned.1.call-start
  83.0 4.5 %all_to_all.16 = bf16[128,4,2048]{2,1,0:T(4,128)(2,1)} reshape(bf16[1,128,8192]{2,1,0:T(8,128)(2,1)} %param.9) | data formatting | bytes 4194304 | tf_op jit(solution)/shard_map/all_to_all | solution.py:79
  87.5 2.7 %copy.27 = bf16[128,4,2048]{2,0,1:T(8,128)(2,1)S(1)} copy(bf16[128,4,2048]{2,1,0:T(4,128)(2,1)} %all_to_all.16) | data formatting | bytes 4194304 | tf_op jit(solution)/shard_map/all_to_all | solution.py:79
  90.3 28.1 %all_to_all.21 = bf16[128,4,2048]{2,0,1:T(8,128)(2,1)S(1)} all-to-all(bf16[128,4,2048]{2,0,1:T(8,128)(2,1)S(1)} %copy.27), channel_id=1, replica_groups=mesh['img'=4,'txt'=8] {'img'}, dimensions={1} | all-to-all | bytes 4194304 | tf_op jit(solution)/shard_map/all_to_all | solution.py:79
  118.4 1.9 copy.49
  120.4 4.3 %copy.31 = bf16[512,16,128]{0,2,1:T(8,128)(2,1)} copy(bf16[512,16,128]{2,1,0:T(8,128)(2,1)} %bitcast.70) | data formatting | bytes 4194304 | tf_op jit(solution)/shard_map/reshape | solution.py:22
  124.7 6.9 %fusion.6 = f32[640,16]{0,1:T(8,128)S(1)} fusion(bf16[640,16,128]{0,2,1:T(8,128)(2,1)S(1)} %multiply_convert_fusion.2, bf16[512,16,128]{0,2,1:T(8,128)(2,1)} %copy.31, bf16[16,640,512]{1,2,0:T(8,128)(2,1)} %copy-done), kind=kOutput, calls=%fused_computation.11 | convolution fusion | flops 1346099200 | bytes 15245312 | tf_op jit(solution)/shard_map/htk,khd->thd/dot_general | solution.py:36
  131.5 12.4 %multiply_convert_fusion = bf16[16,640,512]{1,2,0:T(8,128)(2,1)} fusion(f32[16,640]{1,0:T(8,128)S(1)} %bitcast.72, f32[16,640,512]{1,2,0:T(8,128)} %get-tuple-element.14, f32[16,640]{1,0:T(8,128)S(1)} %get-tuple-element.13, bf16[512,16,128]{0,2,1:T(8,128)(2,1)S(1)} %copy-done.1, bf16[640,16,128]{0,2,1:T(8,128)(2,1)S(1)} %multiply_convert_fusion.2), kind=kOutput, calls=%fused_computation.2 | convolution fusion | flops 1363148800 | bytes 36257792 | tf_op jit(solution)/shard_map/thd,khd->htk/dot_general | solution.py:40
  144.0 10.1 %broadcast_multiply_fusion = f32[16,512,128]{1,2,0:T(8,128)} fusion(bf16[16,640,512]{1,2,0:T(8,128)(2,1)} %multiply_convert_fusion, bf16[640,16,128]{0,2,1:T(8,128)(2,1)} %bitcast.67), kind=kOutput, calls=%fused_computation.15 | convolution fusion | flops 1343225856 | bytes 17301504 | tf_op jit(solution)/shard_map/htk,thd->khd/dot_general | solution.py:61
  154.1 5.5 %copy.37 = f32[512,2048]{1,0:T(8,128)} copy(f32[512,2048]{0,1:T(8,128)} %bitcast.64) | data formatting | bytes 8388608 | tf_op jit(solution)/shard_map/reshape | solution.py:67
  159.5 6.6 %multiply_convert_fusion.1 = bf16[16,128,640]{2,1,0:T(8,128)(2,1)S(1)} fusion(bf16[512,16,128]{0,2,1:T(8,128)(2,1)} %copy.33, bf16[16,640,512]{1,2,0:T(8,128)(2,1)} %multiply_convert_fusion), kind=kOutput, calls=%fused_computation.12 | convolution fusion | flops 1344798720 | bytes 15204352 | tf_op jit(solution)/shard_map/htk,khd->thd/dot_general | solution.py:47
  166.1 2.6 copy.40
  168.7 3.7 %reduce-scatter.5.cloned.1.call-done = f32[64,2048]{1,0:T(8,128)} async-done(((f32[512,2048]{1,0:T(8,128)}), f32[64,2048]{1,0:T(8,128)}) %reduce-scatter.5.cloned.1.call-update) | async-done | bytes 524304 | tf_op jit(solution)/shard_map/reduce_scatter | solution.py:91
  172.5 92.2 %reduce-scatter.3.cloned.1.call-done = f32[64,2048]{1,0:T(8,128)} async-done(((f32[512,2048]{1,0:T(8,128)}), f32[64,2048]{1,0:T(8,128)}) %reduce-scatter.3.cloned.1.call-update) | async-done | bytes 524304 | tf_op jit(solution)/shard_map/reduce_scatter | solution.py:90
  (14 shorter events, 0.0 us)
Async XLA Ops:
  8.8 6.2 %copy-start.4 = (s32[1,8]{1,0:T(1,128)S(1)}, s32[1,8]{1,0:T(1,128)}, u32[]{:S(2)}) copy-start(s32[1,8]{1,0:T(1,128)} %param.12) | copy-start | bytes 100
  8.8 6.3 %copy-start.2 = (bf16[1,640,2048]{2,1,0:T(8,128)(2,1)S(1)}, bf16[1,640,2048]{2,1,0:T(8,128)(2,1)}, u32[]{:S(2)}) copy-start(bf16[1,640,2048]{2,1,0:T(8,128)(2,1)} %param.7) | copy-start | bytes 7864324
  10.5 30.9 %all-to-all-start = ((bf16[4,128,2048]{2,1,0:T(8,128)(2,1)}), bf16[4,128,2048]{2,1,0:T(8,128)(2,1)}, u32[]{:S(2)}, u32[]{:S(2)}) async-start(bf16[4,128,2048]{2,1,0:T(8,128)(2,1)} %pad_maximum_fusion), calls=%async_computation | async-start | bytes 4194304 | tf_op jit(solution)/shard_map/all_to_all | solution.py:77
  15.0 157.5 %reduce-scatter.5.cloned.1.call-start = ((), (), s32[]{:S(2)}) async-start(), calls=%async_computation.5 | async-start | bytes 4718592 | tf_op jit(solution)/shard_map/reduce_scatter | solution.py:91
  17.7 4.9 %copy-start.5 = (f32[1,16]{1,0:T(1,128)S(1)}, f32[1,16]{1,0:T(1,128)}, u32[]{:S(2)}) copy-start(f32[1,16]{1,0:T(1,128)} %param.11) | copy-start | bytes 196
  17.7 4.9 %copy-start.3 = (s32[640]{0:T(1024)S(1)}, s32[640]{0:T(1024)}, u32[]{:S(2)}) copy-start(s32[640]{0:T(1024)} %param.13) | copy-start | bytes 7684
  72.2 5.3 %copy-start = (bf16[16,640,512]{1,2,0:T(8,128)(2,1)}, bf16[16,640,512]{1,2,0:T(8,128)(2,1)S(1)}, u32[]{:S(2)}) copy-start(bf16[16,640,512]{1,2,0:T(8,128)(2,1)S(1)} %fusion.5) | copy-start | bytes 31457284
  83.0 181.7 %reduce-scatter.3.cloned.1.call-start = ((), (), s32[]{:S(2)}) async-start(), calls=%async_computation.4 | async-start | bytes 4718592 | tf_op jit(solution)/shard_map/reduce_scatter | solution.py:90
  124.7 6.9 %copy-start.1 = (bf16[512,16,128]{0,2,1:T(8,128)(2,1)S(1)}, bf16[512,16,128]{0,2,1:T(8,128)(2,1)}, u32[]{:S(2)}) copy-start(bf16[512,16,128]{0,2,1:T(8,128)(2,1)} %copy.31) | copy-start | bytes 6291460
Sparse Core Ops, SparseCore 0:
  83.1 89.3 reduce-scatter.4
  176.7 87.9 reduce-scatter.2
